TPU v7x, 32 devices: a 4x4x1 block of a 4x4x8 slice. The times are simulated.
32 devices in a mesh: spin: 1 (over z), row: 4 (over y), col: 8 (over x, core).
Axes of the slice: x: 4, y: 4, z: 1, core: 2. Of those that a mesh axis runs over, the one named last changes fastest.
The devices are a block of a 4x4x8 slice.
Arguments:
- hamiltonian: float32 [2304, 2304], P(('spin', 'row'), 'col')
- bounds: float32 [2], P('spin')
- n_occ: int32 [1], P('spin')
Outputs:
- output 1: float32 [2304, 2304], P(('spin', 'row'), 'col')
- output 2: float32 [1], P('spin')
All inputs are finite; a program needn't handle non-finite values.
Results may differ from a plain program's by a relative error of at most 0.001.
Values sent between devices are 32-bit elements.
A program may use at most 768 MiB of HBM per device.

v0:
```python
import jax
import jax.numpy as jnp
from jax import lax
from jax.sharding import PartitionSpec as P

STEPS = 3


def solution(mesh):
    n_cols = mesh.shape["col"]
    highest = lax.Precision.HIGHEST

    def local_fn(ham_blk, bounds, n_occ):
        rows_n, cols_n = ham_blk.shape
        mat_order = cols_n * n_cols
        row_ids = lax.axis_index("row") * rows_n + lax.broadcasted_iota(jnp.int32, (rows_n, 1), 0)
        col_ids = lax.axis_index("col") * cols_n + lax.broadcasted_iota(jnp.int32, (1, cols_n), 1)
        diag_mask = row_ids == col_ids
        occupied = n_occ[0].astype(jnp.float32)
        mu_val = lax.psum(jnp.sum(jnp.where(diag_mask, ham_blk, 0.0)), ("row", "col")) / mat_order
        lam_scale = jnp.minimum(occupied / (bounds[1] - mu_val), (mat_order - occupied) / (mu_val - bounds[0]))
        density = jnp.where(diag_mask, (lam_scale * mu_val + occupied) / mat_order, 0.0) - (lam_scale / mat_order) * ham_blk
        for _ in range(STEPS):
            x_rows = lax.all_gather(density, "col", axis=1, tiled=True)
            x_cols = lax.all_gather(density, "row", axis=0, tiled=True)
            dens_sq = jnp.dot(x_rows, x_cols, precision=highest, preferred_element_type=jnp.float32)
            sq_rows = lax.all_gather(dens_sq, "col", axis=1, tiled=True)
            dens_cube = jnp.dot(sq_rows, x_cols, precision=highest, preferred_element_type=jnp.float32)
            part_sums = jnp.stack([jnp.sum(jnp.where(diag_mask, density, 0.0)), jnp.sum(density * density), jnp.sum(dens_sq * density)])
            traces = lax.psum(part_sums, ("row", "col"))
            mix_coef = (traces[1] - traces[2]) / (traces[0] - traces[1])
            density = ((1.0 - 2.0 * mix_coef) * density + (1.0 + mix_coef) * dens_sq - dens_cube) / (1.0 - mix_coef)
        energy = 2.0 * lax.psum(jnp.sum(density * ham_blk), ("row", "col"))
        return density, energy[None]

    spec_mat = P(("spin", "row"), "col")
    return jax.shard_map(local_fn, mesh=mesh, in_specs=(spec_mat, P("spin"), P("spin")), out_specs=(spec_mat, P("spin")), check_vma=False)
```

profile of v0, /device:TPU:97, one launch (start us, length us, event | category | flops | bytes accessed | tf_op | source)
XLA Modules:
  0.0 555.3 jit_solution(12828005620240041457)
XLA Ops:
  7.2 0.0 copy-start.3
  7.2 0.1 all-gather.25.cloned.1.call-start
  8.0 1.4 fusion.11
  9.4 2.0 fusion.3
  11.3 49.7 %psum.35 = f32[]{:T(128)} all-reduce(f32[]{:T(128)} %fusion.3), channel_id=1, replica_groups=mesh['spin'=1,'row'=4,'col'=8] {'row','col'}, use_global_device_ids=true, to_apply=%region_1.2 | all-reduce | flops 1 | bytes 8 | tf_op jit(solution)/shard_map/psum | solution.py:20
  63.0 2.2 fusion.24
  65.3 0.1 all-gather.25.cloned.1.call-update
  65.3 0.1 all-gather.13.cloned.1.call-start
  65.4 0.0 copy-done.3
  65.4 1.0 fusion.4
  66.4 0.1 all-gather.13.cloned.1.call-update
  66.5 0.2 all-gather.15.cloned.1.call-start
  66.7 31.7 %all-gather.25.cloned.1.call-done = f32[4,576,288]{1,2,0:T(8,128)} async-done(((f32[1,576,288]{1,2,0:T(8,128)}), f32[4,576,288]{1,2,0:T(8,128)}) %all-gather.25.cloned.1.call-update) | async-done | bytes 2654224 | tf_op jit(solution)/shard_map/all_gather | solution.py:25
  98.4 5.4 copy.8
  103.8 0.0 copy-start.2
  103.8 3.4 reshape.49
  107.2 30.6 %all-gather.13.cloned.1.call-done = f32[576,2304]{0,1:T(8,128)} async-done(((f32[576,288]{0,1:T(8,128)}), f32[576,2304]{0,1:T(8,128)}) %all-gather.13.cloned.1.call-update) | async-done | bytes 5308432 | tf_op jit(solution)/shard_map/all_gather | solution.py:24
  137.8 0.0 copy-done.2
  137.8 11.0 %fusion.5 = (f32[]{:T(128)}, f32[]{:T(128)}, f32[]{:T(128)}, f32[576,288]{0,1:T(8,128)}) fusion(f32[576,288]{0,1:T(8,128)S(1)} %copy-done.2, s32[576]{0:T(1024)S(1)} %iota_add_fusion, s32[288]{0:T(512)S(1)} %iota_add_fusion.1, f32[576,2304]{0,1:T(8,128)} %all-gather.13.cloned.1.call-done, f32[2304,288]{0,1:T(8,128)S(1)} %reshape.49), kind=kOutput, calls=%fused_computation.13 | convolution fusion | flops 4587632640 | bytes 9293196 | tf_op jit(solution)/shard_map/dot_general | solution.py:26
  148.8 0.1 all-gather.15.cloned.1.call-update
  148.8 0.1 all-gather.27.cloned.1.call-start
  148.9 2.0 pad_maximum_fusion
  150.9 46.0 %psum.36 = f32[3]{0:T(128)S(1)} all-reduce(f32[3]{0:T(128)S(1)} %pad_maximum_fusion), channel_id=1, replica_groups=mesh['spin'=1,'row'=4,'col'=8] {'row','col'}, use_global_device_ids=true, to_apply=%region_5.6 | all-reduce | flops 3 | bytes 24 | tf_op jit(solution)/shard_map/psum | solution.py:30
  196.9 0.7 fusion.10
  200.1 0.0 all-gather.15.cloned.1.call-done
  200.1 10.4 %fusion = f32[576,288]{0,1:T(8,128)} fusion(f32[576,2304]{0,1:T(8,128)} %all-gather.15.cloned.1.call-done, f32[2304,288]{0,1:T(8,128)S(1)} %reshape.49, f32[576,288]{0,1:T(8,128)} %get-tuple-element.22, f32[576,288]{0,1:T(8,128)S(1)} %copy-done.2, f32[]{:T(128)} %bitcast.9, f32[]{:T(128)} %bitcast.8, f32[]{:T(128)} %bitcast.7), kind=kOutput, calls=%fused_computation.8 | convolution fusion | flops 4587300864 | bytes 9953292 | tf_op jit(solution)/shard_map/dot_general | solution.py:28
  210.5 0.1 all-gather.27.cloned.1.call-update
  210.6 0.1 all-gather.17.cloned.1.call-start
  210.7 0.6 all-gather.17.cloned.1.call-update
  211.2 0.5 all-gather.19.cloned.1.call-start
  211.7 32.2 %all-gather.27.cloned.1.call-done = f32[4,576,288]{1,2,0:T(8,128)} async-done(((f32[1,576,288]{1,2,0:T(8,128)}), f32[4,576,288]{1,2,0:T(8,128)}) %all-gather.27.cloned.1.call-update) | async-done | bytes 2654224 | tf_op jit(solution)/shard_map/all_gather | solution.py:25
  243.9 5.4 copy.9
  249.3 0.0 copy-start.1
  249.3 3.4 reshape.51
  252.7 30.5 %all-gather.17.cloned.1.call-done = f32[576,2304]{0,1:T(8,128)} async-done(((f32[576,288]{0,1:T(8,128)}), f32[576,2304]{0,1:T(8,128)}) %all-gather.17.cloned.1.call-update) | async-done | bytes 5308432 | tf_op jit(solution)/shard_map/all_gather | solution.py:24
  283.2 0.0 copy-done.1
  283.2 11.0 %fusion.6 = (f32[]{:T(128)}, f32[]{:T(128)}, f32[]{:T(128)}, f32[576,288]{0,1:T(8,128)}) fusion(f32[576,288]{0,1:T(8,128)S(1)} %copy-done.1, s32[576]{0:T(1024)S(1)} %iota_add_fusion, s32[288]{0:T(512)S(1)} %iota_add_fusion.1, f32[576,2304]{0,1:T(8,128)} %all-gather.17.cloned.1.call-done, f32[2304,288]{0,1:T(8,128)S(1)} %reshape.51), kind=kOutput, calls=%fused_computation.14 | convolution fusion | flops 4587632640 | bytes 9293196 | tf_op jit(solution)/shard_map/dot_general | solution.py:26
  294.2 0.1 all-gather.19.cloned.1.call-update
  294.2 0.1 all-gather.29.cloned.1.call-start
  294.3 2.0 pad_maximum_fusion.1
  296.3 45.9 %psum.37 = f32[3]{0:T(128)S(1)} all-reduce(f32[3]{0:T(128)S(1)} %pad_maximum_fusion.1), channel_id=1, replica_groups=mesh['spin'=1,'row'=4,'col'=8] {'row','col'}, use_global_device_ids=true, to_apply=%region_9.10 | all-reduce | flops 3 | bytes 24 | tf_op jit(solution)/shard_map/psum | solution.py:30
  342.2 0.7 fusion.9
  345.4 0.0 all-gather.19.cloned.1.call-done
  345.4 10.4 %fusion.1 = f32[576,288]{0,1:T(8,128)} fusion(f32[576,2304]{0,1:T(8,128)} %all-gather.19.cloned.1.call-done, f32[2304,288]{0,1:T(8,128)S(1)} %reshape.51, f32[576,288]{0,1:T(8,128)} %get-tuple-element.23, f32[576,288]{0,1:T(8,128)S(1)} %copy-done.1, f32[]{:T(128)} %bitcast.16, f32[]{:T(128)} %bitcast.15, f32[]{:T(128)} %bitcast.14), kind=kOutput, calls=%fused_computation.9 | convolution fusion | flops 4587300864 | bytes 9953292 | tf_op jit(solution)/shard_map/dot_general | solution.py:28
  355.9 0.1 all-gather.29.cloned.1.call-update
  355.9 0.1 all-gather.21.cloned.1.call-start
  356.0 0.7 all-gather.21.cloned.1.call-update
  356.8 0.3 all-gather.23.cloned.1.call-start
  357.0 32.2 %all-gather.29.cloned.1.call-done = f32[4,576,288]{1,2,0:T(8,128)} async-done(((f32[1,576,288]{1,2,0:T(8,128)}), f32[4,576,288]{1,2,0:T(8,128)}) %all-gather.29.cloned.1.call-update) | async-done | bytes 2654224 | tf_op jit(solution)/shard_map/all_gather | solution.py:25
  389.3 5.4 copy.10
  394.6 0.0 copy-start
  394.6 3.4 reshape.53
  398.1 30.6 %all-gather.21.cloned.1.call-done = f32[576,2304]{0,1:T(8,128)} async-done(((f32[576,288]{0,1:T(8,128)}), f32[576,2304]{0,1:T(8,128)}) %all-gather.21.cloned.1.call-update) | async-done | bytes 5308432 | tf_op jit(solution)/shard_map/all_gather | solution.py:24
  428.7 0.0 copy-done
  428.7 11.0 %fusion.7 = (f32[]{:T(128)}, f32[]{:T(128)}, f32[]{:T(128)}, f32[576,288]{0,1:T(8,128)}) fusion(f32[576,288]{0,1:T(8,128)S(1)} %copy-done, s32[576]{0:T(1024)S(1)} %iota_add_fusion, s32[288]{0:T(512)S(1)} %iota_add_fusion.1, f32[576,2304]{0,1:T(8,128)} %all-gather.21.cloned.1.call-done, f32[2304,288]{0,1:T(8,128)S(1)} %reshape.53), kind=kOutput, calls=%fused_computation.15 | convolution fusion | flops 4587632640 | bytes 9293196 | tf_op jit(solution)/shard_map/dot_general | solution.py:26
  439.7 0.1 all-gather.23.cloned.1.call-update
  439.7 2.0 pad_maximum_fusion.2
  441.7 46.0 %psum.38 = f32[3]{0:T(128)S(1)} all-reduce(f32[3]{0:T(128)S(1)} %pad_maximum_fusion.2), channel_id=1, replica_groups=mesh['spin'=1,'row'=4,'col'=8] {'row','col'}, use_global_device_ids=true, to_apply=%region_13.14 | all-reduce | flops 3 | bytes 24 | tf_op jit(solution)/shard_map/psum | solution.py:30
  487.7 0.7 fusion.8
  490.9 0.0 all-gather.23.cloned.1.call-done
  491.0 11.3 %multiply_reduce_fusion = (f32[]{:T(128)}, f32[576,288]{0,1:T(8,128)}) fusion(f32[576,288]{0,1:T(8,128)} %param.3, f32[]{:T(128)} %bitcast.23, f32[576,2304]{0,1:T(8,128)} %all-gather.23.cloned.1.call-done, f32[2304,288]{0,1:T(8,128)S(1)} %reshape.53, f32[576,288]{0,1:T(8,128)} %get-tuple-element.24, f32[]{:T(128)} %bitcast.22, f32[576,288]{0,1:T(8,128)S(1)} %copy-done, ...), kind=kOutput, calls=%fused_computation.16 | convolution fusion | flops 4587632640 | bytes 10616848 | tf_op jit(solution)/shard_map/dot_general | solution.py:28
  502.3 44.4 %psum.39 = f32[]{:T(128)} all-reduce(f32[]{:T(128)} %get-tuple-element.25), channel_id=1, replica_groups=mesh['spin'=1,'row'=4,'col'=8] {'row','col'}, use_global_device_ids=true, to_apply=%region_15.16 | all-reduce | flops 1 | bytes 8 | tf_op jit(solution)/shard_map/psum | solution.py:33
  (2 shorter events, 0.0 us)
Async XLA Ops:
  7.2 58.2 %copy-start.3 = (f32[576,288]{0,1:T(8,128)S(1)}, f32[576,288]{0,1:T(8,128)}, u32[]{:S(2)}) copy-start(f32[576,288]{0,1:T(8,128)} %param.3) | copy-start | bytes 1990660
  7.2 91.2 %all-gather.25.cloned.1.call-start = ((), (), s32[]{:S(2)}) async-start(), calls=%async_computation.6 | async-start | bytes 3686400 | tf_op jit(solution)/shard_map/all_gather | solution.py:25
  65.3 72.5 %all-gather.13.cloned.1.call-start = ((), (), s32[]{:S(2)}) async-start(), calls=%async_computation | async-start | bytes 6635520 | tf_op jit(solution)/shard_map/all_gather | solution.py:24
  66.5 133.6 %all-gather.15.cloned.1.call-start = ((), (), s32[]{:S(2)}) async-start(), calls=%async_computation.1 | async-start | bytes 6635520 | tf_op jit(solution)/shard_map/all_gather | solution.py:27
  103.8 34.0 %copy-start.2 = (f32[576,288]{0,1:T(8,128)S(1)}, f32[576,288]{0,1:T(8,128)}, u32[]{:S(2)}) copy-start(f32[576,288]{0,1:T(8,128)} %fusion.4) | copy-start | bytes 1990660
  148.8 95.1 %all-gather.27.cloned.1.call-start = ((), (), s32[]{:S(2)}) async-start(), calls=%async_computation.7 | async-start | bytes 3686400 | tf_op jit(solution)/shard_map/all_gather | solution.py:25
  210.6 72.6 %all-gather.17.cloned.1.call-start = ((), (), s32[]{:S(2)}) async-start(), calls=%async_computation.2 | async-start | bytes 6635520 | tf_op jit(solution)/shard_map/all_gather | solution.py:24
  211.2 134.2 %all-gather.19.cloned.1.call-start = ((), (), s32[]{:S(2)}) async-start(), calls=%async_computation.3 | async-start | bytes 6635520 | tf_op jit(solution)/shard_map/all_gather | solution.py:27
  249.3 33.9 %copy-start.1 = (f32[576,288]{0,1:T(8,128)S(1)}, f32[576,288]{0,1:T(8,128)}, u32[]{:S(2)}) copy-start(f32[576,288]{0,1:T(8,128)} %fusion) | copy-start | bytes 1990660
  294.2 95.0 %all-gather.29.cloned.1.call-start = ((), (), s32[]{:S(2)}) async-start(), calls=%async_computation.8 | async-start | bytes 3686400 | tf_op jit(solution)/shard_map/all_gather | solution.py:25
  355.9 72.7 %all-gather.21.cloned.1.call-start = ((), (), s32[]{:S(2)}) async-start(), calls=%async_computation.4 | async-start | bytes 6635520 | tf_op jit(solution)/shard_map/all_gather | solution.py:24
  356.8 134.2 %all-gather.23.cloned.1.call-start = ((), (), s32[]{:S(2)}) async-start(), calls=%async_computation.5 | async-start | bytes 6635520 | tf_op jit(solution)/shard_map/all_gather | solution.py:27
  394.6 34.0 %copy-start = (f32[576,288]{0,1:T(8,128)S(1)}, f32[576,288]{0,1:T(8,128)}, u32[]{:S(2)}) copy-start(f32[576,288]{0,1:T(8,128)} %fusion.1) | copy-start | bytes 1990660
Sparse Core Ops, SparseCore 0:
  65.4 32.8 all-gather.24
  100.5 37.2 all-gather.12
  149.0 37.3 all-gather.14
  210.7 33.1 all-gather.26
  245.9 37.2 all-gather.16
  294.4 37.3 all-gather.18
  356.1 33.1 all-gather.28
  391.4 37.2 all-gather.20
  439.8 37.3 all-gather.22
where the time goes:
time: 559 us; the launch traced here: 555 us
  blocking collectives  232 us (42%)
  waiting for transfers between devices  190 us (34%)
  matrix products  65.1 us (12%)
  local copies, waits for them, and re-layouts  29.8 us (5%)
  between operations  26.3 us (5%)
  other arithmetic  11.2 us (2%)
    psum x3, blocking collectives, local_fn(): traces = lax.psum(part_sums, ('row', 'col'))  138 us
    all_gather x3, waiting for transfers between devices, local_fn(): x_cols = lax.all_gather(density, 'row', axis=0, tiled=True)  96.1 us
    all_gather x3, waiting for transfers between devices, local_fn(): x_rows = lax.all_gather(density, 'col', axis=1, tiled=True)  91.7 us
    psum x1, blocking collectives, local_fn(): lax.psum(jnp.sum(jnp.where(diag_mask, ham_blk, 0.0)), ('row', 'col'))  49.7 us
    psum x1, blocking collectives, local_fn(): energy = 2.0 * lax.psum(jnp.sum(density * ham_blk), ('row', 'col'))  44.4 us
    dot_general x3, matrix products, local_fn(): jnp.dot(x_rows, x_cols, precision=highest, preferred_element_type=jnp.flo...  33 us
    dot_general x3, matrix products, local_fn(): jnp.dot(sq_rows, x_cols, precision=highest, preferred_element_type=jnp.fl...  32.2 us
    all_gather x3, local copies, waits for them, and re-layouts, local_fn(): x_cols = lax.all_gather(density, 'row', axis=0, tiled=True)  16.1 us
  transfers between devices with their start and end apart: 9, of which 6 were waited for; matrix products, arithmetic and copies ran while one was open for 6% of the time, Pallas kernels for 0%

commit v1 on v0

v1 whole, which is shorter than its diff:
```python
import functools

import jax
import jax.numpy as jnp
from jax import lax
from jax.experimental import pallas as pl
from jax.experimental.pallas import tpu as pltpu
from jax.sharding import PartitionSpec as P

STEPS = 3
TILE = 256
LANES = 128
HIGHEST = lax.Precision.HIGHEST
MESH = pl.DeviceIdType.MESH

BACK1, FRONT1, OPP1, BACK2, FRONT2, OPP2, TWIN_OWN, TWIN_BACK, TWIN_FRONT, TWIN_OPP = range(10)


def dot_nn(a, b):
    return lax.dot_general(a, b, (((1,), (0,)), ((), ())), precision=HIGHEST, preferred_element_type=jnp.float32)


def dot_nt(a, b):
    return lax.dot_general(a, b, (((1,), (1,)), ((), ())), precision=HIGHEST, preferred_element_type=jnp.float32)


def total(v):
    return jnp.sum(jnp.sum(jnp.sum(v, axis=0), axis=0, keepdims=True), axis=1, keepdims=True)


def kernel(
    ny, nx, bounds_ref, occ_ref, ham_ref, dens_ref, energy_ref,
    store, slots, out_slots, out_blk, h_pan, x_pan, x2_pan, x3_pan, red,
    in_send, in_recv, out_send, out_recv, red_send, red_recv, g_send, g_recv,
):
    n_cols = 2 * nx
    n_dev = ny * n_cols
    rows_n, cols_n = ham_ref.shape
    order = cols_n * n_cols
    groups = order // TILE
    window = (groups + 1) // 2
    rpd = order // n_dev
    my_y = lax.axis_index("row")
    my_m = lax.axis_index("col")
    my_x, my_c = my_m // 2, lax.rem(my_m, 2)
    flat = store.reshape(2, window, 2, order, LANES)

    def dev(y, x, c):
        return {"row": y, "col": 2 * x + c}

    x_front, x_back, x_opp = (lax.rem(my_x + d + 2 * my_c, nx) for d in (1, 3, 2))
    x_opp = lax.rem(my_x + 2, nx)
    y_front, y_back = (lax.rem(my_y + d + 2 * my_c, ny) for d in (1, 3))
    y_opp = lax.rem(my_y + 2, ny)

    barrier = pltpu.get_barrier_semaphore()
    me = my_y * n_cols + my_m

    def sig(k, carry):
        t = lax.rem(me + k, n_dev)
        pl.semaphore_signal(barrier, inc=1, device_id={"row": t // n_cols, "col": lax.rem(t, n_cols)}, device_id_type=MESH)
        return carry

    lax.fori_loop(1, n_dev, sig, 0)

    row_id = my_y * rows_n + lax.broadcasted_iota(jnp.int32, (rows_n, cols_n), 0)
    col_id = my_m * cols_n + lax.broadcasted_iota(jnp.int32, (rows_n, cols_n), 1)
    tr_h = jnp.sum(jnp.sum(jnp.where(row_id == col_id, ham_ref[...], 0.0), axis=0, keepdims=True), axis=1, keepdims=True)
    lane = lax.broadcasted_iota(jnp.int32, (1, LANES), 1)

    def red_start(use, sums):
        row = jnp.zeros((1, LANES), jnp.float32)
        for q, s in enumerate(sums):
            row = jnp.where(lane == q, s, row)
        red[use, me] = row

        def push(k, carry):
            t = lax.rem(me + k, n_dev)
            pltpu.make_async_remote_copy(
                red.at[use, me], red.at[use, me], red_send.at[use], red_recv.at[use],
                device_id={"row": t // n_cols, "col": lax.rem(t, n_cols)}, device_id_type=MESH,
            ).start()
            return carry

        lax.fori_loop(1, n_dev, push, 0)

    def red_wait(use, count):
        many = red.at[use, pl.ds(0, n_dev - 1)]
        copy = pltpu.make_async_remote_copy(many, many, red_send.at[use], red_recv.at[use], device_id=dev(my_y, my_x, my_c), device_id_type=MESH)
        copy.wait_recv()
        copy.wait_send()
        row = jnp.sum(red[use], axis=0)
        return [jnp.sum(jnp.where(lane == q, row, 0.0), axis=1, keepdims=True) for q in range(count)]

    pl.semaphore_wait(barrier, n_dev - 1)
    red_start(0, [tr_h])

    def in_copy(m_to):
        r = pl.multiple_of(lax.rem(m_to, 2) * cols_n + (m_to // 2) * rpd, 8)
        return pltpu.make_async_remote_copy(
            ham_ref.at[pl.ds(r, rpd), :], slots.at[my_m], in_send.at[m_to], in_recv.at[my_m],
            device_id={"row": my_y, "col": m_to}, device_id_type=MESH,
        )

    def in_wait(m_from):
        return pltpu.make_async_remote_copy(
            slots.at[m_from], slots.at[m_from], in_send.at[m_from], in_recv.at[m_from],
            device_id={"row": my_y, "col": my_m}, device_id_type=MESH,
        )

    for k in range(1, n_cols):
        in_copy(lax.rem(my_m + k, n_cols)).start()
    slots[my_m] = ham_ref[pl.ds(pl.multiple_of(my_c * cols_n + my_x * rpd, 8), rpd), :]
    for k in range(1, n_cols):
        in_wait(lax.rem(my_m + k, n_cols)).wait_recv()

    panel = jnp.concatenate([slots[2 * (k % ny) + k // ny] for k in range(n_cols)], axis=1)
    for g in range(groups):
        h_pan[g] = panel[:, g * TILE:(g + 1) * TILE]

    first_row = rpd * (4 * (ny * my_c + my_y) + my_x)
    shape3 = (groups, rpd, TILE)
    diag = (first_row + lax.broadcasted_iota(jnp.int32, shape3, 1)) == (
        TILE * lax.broadcasted_iota(jnp.int32, shape3, 0) + lax.broadcasted_iota(jnp.int32, shape3, 2)
    )
    occupied = jnp.full((1, 1), occ_ref[0], jnp.int32).astype(jnp.float32)
    eps_min = jnp.full((1, 1), bounds_ref[0], jnp.float32)
    eps_max = jnp.full((1, 1), bounds_ref[1], jnp.float32)
    mu = red_wait(0, 1)[0] / order
    lam = jnp.minimum(occupied / (eps_max - mu), (order - occupied) / (mu - eps_min))
    x_pan[...] = jnp.where(diag, ((lam * mu + occupied) / order)[None], 0.0) - (lam / order)[None] * h_pan[...]

    group0 = first_row // TILE
    split = TILE * (group0 + 1) - first_row
    upper = lax.broadcasted_iota(jnp.int32, (rpd, TILE), 0) < split

    def step_body(step, carry):
        par = lax.rem(step, 2)

        def region(kind, chunk, half):
            at = store.at[par, chunk, half]
            if kind in (BACK1, FRONT1, OPP1, "own1"):
                x = {BACK1: x_back, FRONT1: x_front, OPP1: x_opp, "own1": my_x}[kind] if half == 0 else my_x
                y = {BACK1: y_back, FRONT1: y_front, OPP1: y_opp, "own1": my_y}[kind] if half == 1 else my_y
                return at.at[my_c, y, x]
            base = {TWIN_OWN: "own2", TWIN_BACK: BACK2, TWIN_FRONT: FRONT2, TWIN_OPP: OPP2}.get(kind, kind)
            if half == 0:
                return at.at[my_c, {BACK2: y_back, FRONT2: y_front, OPP2: y_opp, "own2": my_y}[base]]
            return at.at[my_c, :, {BACK2: x_back, FRONT2: x_front, OPP2: x_opp, "own2": my_x}[base]]

        def twin_region(kind, chunk, half):
            at = store.at[par, chunk, half]
            if half == 0:
                return at.at[1 - my_c, {TWIN_OWN: my_y, TWIN_BACK: y_front, TWIN_FRONT: y_back, TWIN_OPP: y_opp}[kind]]
            return at.at[1 - my_c, :, {TWIN_OWN: my_x, TWIN_BACK: x_front, TWIN_FRONT: x_back, TWIN_OPP: x_opp}[kind]]

        def target(kind, half):
            if kind >= TWIN_OWN:
                return dev(my_y, my_x, 1 - my_c)
            along_x = (half == 0) == (kind in (BACK1, FRONT1, OPP1))
            front = kind in (BACK1, OPP1, BACK2, OPP2)
            if along_x:
                return dev(my_y, x_front if front else x_back, my_c)
            return dev(y_front if front else y_back, my_x, my_c)

        def message(kind, chunk, half):
            src = region(
                {BACK1: "own1", FRONT1: "own1", OPP1: BACK1, BACK2: "own2", FRONT2: "own2", OPP2: BACK2}.get(kind, kind), chunk, half
            )
            hc = 2 * chunk + half
            return pltpu.make_async_remote_copy(
                src, src, g_send.at[hc, kind], g_recv.at[hc, kind], device_id=target(kind, half), device_id_type=MESH
            )

        def arrival(kind, chunk, half):
            dst = twin_region(kind, chunk, half) if kind >= TWIN_OWN else region(kind, chunk, half)
            hc = 2 * chunk + half
            return pltpu.make_async_remote_copy(
                dst, dst, g_send.at[hc, kind], g_recv.at[hc, kind], device_id=dev(my_y, my_x, my_c), device_id_type=MESH
            )

        def send(kind, chunk):
            for half in (0, 1):
                message(kind, chunk, half).start()

        def recv(kind, chunk):
            for half in (0, 1):
                arrival(kind, chunk, half).wait_recv()

        for chunk in range(window):
            piece = jnp.where(upper, x_pan[lax.rem(group0 + chunk, groups)], x_pan[lax.rem(group0 + 1 + chunk, groups)])
            for half in (0, 1):
                store[par, chunk, half, my_c, my_y, my_x] = piece[:, half * LANES:(half + 1) * LANES]
            send(BACK1, chunk)
            send(FRONT1, chunk)

        for g in range(groups):
            x2_pan[g] = jnp.zeros((rpd, TILE), jnp.float32)

        for chunk in range(window):
            recv(BACK1, chunk)
            send(OPP1, chunk)

        def spread(chunk):
            recv(FRONT1, chunk)
            recv(OPP1, chunk)
            send(BACK2, chunk)
            send(FRONT2, chunk)
            send(TWIN_OWN, chunk)

        def relay(chunk):
            recv(BACK2, chunk)
            send(OPP2, chunk)
            send(TWIN_BACK, chunk)

        def block(chunk, a):
            rows = pl.ds(pl.multiple_of(a * TILE, TILE), TILE)
            return jnp.concatenate([flat[par, chunk, 0, rows, :], flat[par, chunk, 1, rows, :]], axis=1)

        spread(0)
        spread(1)
        relay(0)
        for chunk in range(window):
            if chunk + 2 < window:
                spread(chunk + 2)
            if chunk + 1 < window:
                relay(chunk + 1)
            recv(FRONT2, chunk)
            send(TWIN_FRONT, chunk)
            recv(OPP2, chunk)
            send(TWIN_OPP, chunk)
            for kind in (TWIN_OWN, TWIN_BACK, TWIN_FRONT, TWIN_OPP):
                recv(kind, chunk)

            def gather_mul(a, carry, chunk=chunk):
                w = block(chunk, a)
                h = lax.rem(a + chunk, groups)
                x2_pan[h] += dot_nn(x_pan[a], w)
                if chunk:
                    x2_pan[a] += dot_nt(x_pan[h], w)
                return carry

            lax.fori_loop(0, groups, gather_mul, 0, unroll=3)

        x = x_pan[...]
        x2 = x2_pan[...]
        red_start(1 + step, [total(jnp.where(diag, x, 0.0)), total(x * x), total(x2 * x)])

        def cube(h, carry):
            acc = None
            for d in range(window):
                g = lax.rem(h + groups - d, groups)
                part = dot_nn(x2_pan[g], block(d, g))
                acc = part if acc is None else acc + part
            for d in range(1, window):
                acc = acc + dot_nt(x2_pan[lax.rem(h + d, groups)], block(d, h))
            x3_pan[h] = acc
            return carry

        lax.fori_loop(0, groups, cube, 0)

        t1, t2, t3 = red_wait(1 + step, 3)
        c = (t2 - t3) / (t1 - t2)
        x_pan[...] = ((1.0 - 2.0 * c)[None] * x_pan[...] + (1.0 + c)[None] * x2_pan[...] - x3_pan[...]) / (1.0 - c)[None]

        for chunk in range(window):
            for kind in range(10):
                for half in (0, 1):
                    message(kind, chunk, half).wait_send()
        return carry

    lax.fori_loop(0, STEPS, step_body, 0)

    red_start(1 + STEPS, [total(x_pan[...] * h_pan[...])])
    result = jnp.concatenate([x_pan[g] for g in range(groups)], axis=1)
    for k in range(n_cols):
        out_slots[2 * (k % ny) + k // ny] = result[:, k * cols_n:(k + 1) * cols_n]

    my_rows = pl.ds(pl.multiple_of(my_c * cols_n + my_x * rpd, 8), rpd)

    def out_copy(m_to):
        return pltpu.make_async_remote_copy(
            out_slots.at[m_to], out_blk.at[my_rows, :], out_send.at[m_to], out_recv.at[my_m],
            device_id={"row": my_y, "col": m_to}, device_id_type=MESH,
        )

    def out_wait(m_from):
        r = pl.ds(pl.multiple_of(lax.rem(m_from, 2) * cols_n + (m_from // 2) * rpd, 8), rpd)
        return pltpu.make_async_remote_copy(
            out_blk.at[r, :], out_blk.at[r, :], out_send.at[m_from], out_recv.at[m_from],
            device_id={"row": my_y, "col": my_m}, device_id_type=MESH,
        )

    for k in range(1, n_cols):
        out_copy(lax.rem(my_m + k, n_cols)).start()
    out_blk[my_rows, :] = out_slots[my_m]
    for k in range(1, n_cols):
        out_wait(lax.rem(my_m + k, n_cols)).wait_recv()
    dens_ref[...] = out_blk[...]
    energy_ref[...] = 2.0 * red_wait(1 + STEPS, 1)[0]
    for k in range(1, n_cols):
        in_copy(lax.rem(my_m + k, n_cols)).wait_send()
        out_copy(lax.rem(my_m + k, n_cols)).wait_send()


def solution(mesh):
    ny, n_cols = mesh.shape["row"], mesh.shape["col"]
    nx = n_cols // 2
    n_dev = ny * n_cols

    def local_fn(ham_blk, bounds, n_occ):
        rows_n, cols_n = ham_blk.shape
        order = cols_n * n_cols
        groups = order // TILE
        window = (groups + 1) // 2
        rpd = order // n_dev
        dens, energy = pl.pallas_call(
            functools.partial(kernel, ny, nx),
            out_shape=(jax.ShapeDtypeStruct((rows_n, cols_n), jnp.float32), jax.ShapeDtypeStruct((1, 1), jnp.float32)),
            in_specs=[pl.BlockSpec(memory_space=pltpu.SMEM)] * 2 + [pl.BlockSpec(memory_space=pltpu.VMEM)],
            out_specs=(pl.BlockSpec(memory_space=pltpu.VMEM),) * 2,
            scratch_shapes=[
                pltpu.VMEM((2, window, 2, 2, ny, nx, rpd, LANES), jnp.float32),
                pltpu.VMEM((n_cols, rpd, cols_n), jnp.float32),
                pltpu.VMEM((n_cols, rpd, cols_n), jnp.float32),
                pltpu.VMEM((rows_n, cols_n), jnp.float32),
                pltpu.VMEM((groups, rpd, TILE), jnp.float32),
                pltpu.VMEM((groups, rpd, TILE), jnp.float32),
                pltpu.VMEM((groups, rpd, TILE), jnp.float32),
                pltpu.VMEM((groups, rpd, TILE), jnp.float32),
                pltpu.VMEM((STEPS + 2, n_dev, 1, LANES), jnp.float32),
                pltpu.SemaphoreType.DMA((n_cols,)),
                pltpu.SemaphoreType.DMA((n_cols,)),
                pltpu.SemaphoreType.DMA((n_cols,)),
                pltpu.SemaphoreType.DMA((n_cols,)),
                pltpu.SemaphoreType.DMA((STEPS + 2,)),
                pltpu.SemaphoreType.DMA((STEPS + 2,)),
                pltpu.SemaphoreType.DMA((2 * window, 10)),
                pltpu.SemaphoreType.DMA((2 * window, 10)),
            ],
            compiler_params=pltpu.CompilerParams(collective_id=0, has_side_effects=True, vmem_limit_bytes=58 * 1024 * 1024),
            name="purify",
        )(bounds, n_occ, ham_blk)
        return dens, energy.reshape(1)

    spec_mat = P(("spin", "row"), "col")
    return jax.shard_map(local_fn, mesh=mesh, in_specs=(spec_mat, P("spin"), P("spin")), out_specs=(spec_mat, P("spin")), check_vma=False)
```

time: 559 us -> 235 us (0.42)
  blocking collectives: 232 us -> 0 us
  Pallas kernels: 0 us -> 227 us
  waiting for transfers between devices: 190 us -> 0 us
  matrix products: 65.1 us -> 0 us
  local copies, waits for them, and re-layouts: 29.8 us -> 4.7 us
  between operations: 26.3 us -> 3.02 us
  other arithmetic: 11.2 us -> 0 us
    psum x5 -> x0, blocking collectives: 232 us -> none  [the longest x3 138 us: local_fn(): traces = lax.psum(part_sums, ('row', 'col'))]
    pallas_call x0 -> x1, Pallas kernels: none -> 227 us  [local_fn(): pl.pallas_call(functools.partial(kernel, ny, nx), out_shape=(jax.ShapeDty...]
    all_gather x9 -> x0, waiting for transfers between devices: 188 us -> none  [the longest x3 96.1 us: local_fn(): x_cols = lax.all_gather(density, 'row', axis=0, tiled=True)]
    dot_general x6 -> x0, matrix products: 65.1 us -> none  [the longest x3 33 us: local_fn(): jnp.dot(x_rows, x_cols, precision=highest, preferred_element_type=jnp.flo...]
    all_gather x3 -> x0, local copies, waits for them, and re-layouts: 16.1 us -> none  [local_fn(): x_cols = lax.all_gather(density, 'row', axis=0, tiled=True)]
    another operation x3 -> x0, other arithmetic: 5.95 us -> none  [local_fn(): jnp.stack([jnp.sum(jnp.where(diag_mask, density, 0.0)), jnp.sum(density *...]
  transfers between devices with their start and end apart: 9 -> 0, of which waited for: 6 -> 0; matrix products, arithmetic and copies ran while one was open for 6% -> 0% of each run, Pallas kernels for 0% -> 0%
where the time goes in v1:
time: 235 us
  Pallas kernels  227 us (97%)
  local copies, waits for them, and re-layouts  4.7 us (2%)
  between operations  3.02 us (1%)
    pallas_call x1, Pallas kernels, local_fn(): pl.pallas_call(functools.partial(kernel, ny, nx), out_shape=(jax.ShapeDty...  227 us

profile of v1, /device:TPU:97, one launch (start us, length us, event | category | flops | bytes accessed | tf_op | source)
XLA Modules:
  0.0 234.7 jit_solution(9526864655443038117)
XLA Ops:
  1.3 2.4 %copy.5.ham_ref = f32[576,288]{1,0:T(8,128)} copy(f32[576,288]{0,1:T(8,128)} %param.3) | data formatting | bytes 1327104 | tf_op args[0]
  3.6 227.0 %purify.1 = (f32[576,288]{1,0:T(8,128)}, f32[1,1]{1,0:T(1,128)}) custom-call(f32[2]{0:T(128)} %bounds_ref.1, s32[1]{0:T(128)S(6)} %copy.8.occ_ref, f32[576,288]{1,0:T(8,128)} %copy.5.ham_ref), custom_call_target="tpu_custom_call" | custom-call | tf_op jit(solution)/shard_map/purify/pallas_call | solution.py:317
  230.6 2.3 copy.6
